TPU v7x, 32 devices: a whole 2x2x4 slice. The times are simulated.
32 devices in a mesh: batch: 4 (over x, core), seq: 8 (over z, y).
Axes of the slice: x: 2, y: 2, z: 4, core: 2. Of those that a mesh axis runs over, the one named last changes fastest.
Arguments:
- signal: bfloat16 [4, 2048, 256], P('batch', 'seq'), may hold values from -0.3125 to 0.3125
- grad_out: bfloat16 [4, 2048, 256], P('batch', 'seq'), may hold values from -6 to 6
- filter_taps: float32 [2048, 256], P('seq'), may hold values from -0.3125 to 0.3125
- skip_gain: float32 [256], replicated, may hold values from 0.5 to 2
Outputs:
- input_grad: bfloat16 [4, 2048, 256], P('batch', 'seq')
- filter_grad: float32 [2048, 256], P('seq')
All inputs are finite; a program needn't handle non-finite values.
Results may differ from a plain program's by a relative error of at most 0.001.
Values sent between devices are 32-bit elements; how exact they have to be, the bound alone decides.
A program may use at most 64 MiB of HBM per device.

v0:
```python
import jax
import jax.numpy as jnp
from jax import lax
from jax.sharding import PartitionSpec as P


def angle_table(height, width, period):
    product = lax.broadcasted_iota(jnp.int32, (height, width), 0) * lax.broadcasted_iota(
        jnp.int32, (height, width), 1
    )
    return 2.0 * jnp.pi / period * (product % period).astype(jnp.float32)


def angle_of(product, period):
    return 2.0 * jnp.pi / period * (product % period).astype(jnp.float32)


def coarse_order(slot, seq_count):
    pair_index = slot // 2
    odd_slot = slot % 2
    return jnp.where(
        pair_index == 0,
        odd_slot * seq_count,
        jnp.where(odd_slot == 0, pair_index, 2 * seq_count - pair_index),
    )


def contract(form, table, operand):
    return jnp.einsum(form, table, operand, precision=lax.Precision.HIGHEST)


def forward_spectra(columns):
    seq_count = lax.axis_size("seq")
    row_count = columns.shape[0]
    part_rows = row_count // seq_count
    period_len = 2 * row_count * seq_count
    spread = lax.all_to_all(
        columns.reshape(1, row_count, columns.shape[1]),
        "seq",
        split_axis=1,
        concat_axis=0,
        tiled=True,
    )
    slot_grid = lax.broadcasted_iota(jnp.int32, (2 * seq_count, seq_count), 0)
    source_grid = lax.broadcasted_iota(jnp.int32, (2 * seq_count, seq_count), 1)
    first_table = angle_of(coarse_order(slot_grid, seq_count) * source_grid, 2 * seq_count)
    cos_first = jnp.cos(first_table)
    sin_first = jnp.sin(first_table)
    half_width = spread.shape[2] // 2
    real_in = spread[:, :, :half_width]
    imag_in = spread[:, :, half_width:]
    real_part = contract("ks,srw->krw", cos_first, real_in) + contract(
        "ks,srw->krw", sin_first, imag_in
    )
    imag_part = contract("ks,srw->krw", cos_first, imag_in) - contract(
        "ks,srw->krw", sin_first, real_in
    )
    global_row = lax.axis_index("seq") * part_rows + lax.broadcasted_iota(
        jnp.int32, (2 * seq_count, part_rows), 1
    )
    coarse = coarse_order(lax.broadcasted_iota(jnp.int32, (2 * seq_count, part_rows), 0), seq_count)
    phases = angle_of(global_row * coarse, period_len)
    cos_turn = jnp.cos(phases)[:, :, None]
    sin_turn = jnp.sin(phases)[:, :, None]
    rotated = jnp.stack(
        [real_part * cos_turn + imag_part * sin_turn, imag_part * cos_turn - real_part * sin_turn]
    )
    inner_table = angle_table(row_count, row_count, row_count)
    cos_inner = jnp.cos(inner_table)
    sin_inner = jnp.sin(inner_table)
    pieces = lax.all_to_all(rotated, "seq", split_axis=1, concat_axis=2, tiled=True)
    real_sum = contract("qr,krw->kqw", cos_inner, pieces[0]) + contract(
        "qr,krw->kqw", sin_inner, pieces[1]
    )
    imag_sum = contract("qr,krw->kqw", cos_inner, pieces[1]) - contract(
        "qr,krw->kqw", sin_inner, pieces[0]
    )
    return jnp.stack([real_sum, imag_sum])


def split_pairs(packed):
    reversed_q = packed[:, :, ::-1]
    zero_row = jnp.roll(reversed_q[:, 0], 1, axis=1)
    own_pair = jnp.stack([zero_row, reversed_q[:, 1]], axis=1)
    partner = jnp.where(lax.axis_index("seq") == 0, own_pair, reversed_q[:, ::-1])
    first = jnp.stack([0.5 * (packed[0] + partner[0]), 0.5 * (packed[1] - partner[1])])
    second = jnp.stack([0.5 * (packed[1] + partner[1]), 0.5 * (partner[0] - packed[0])])
    return (first, second)


def inverse_rows(spectra):
    seq_count = lax.axis_size("seq")
    row_count = spectra.shape[2]
    period_len = 2 * row_count * seq_count
    inner_table = angle_table(row_count, row_count, row_count)
    cos_inner = jnp.cos(inner_table)
    sin_inner = jnp.sin(inner_table)
    real_sum = contract("qr,krw->kqw", cos_inner, spectra[0]) - contract(
        "qr,krw->kqw", sin_inner, spectra[1]
    )
    imag_sum = contract("qr,krw->kqw", cos_inner, spectra[1]) + contract(
        "qr,krw->kqw", sin_inner, spectra[0]
    )
    coarse = coarse_order(
        2 * lax.axis_index("seq") + lax.broadcasted_iota(jnp.int32, (2, row_count), 0), seq_count
    )
    position = lax.broadcasted_iota(jnp.int32, (2, row_count), 1)
    phases = angle_of(position * coarse, period_len)
    cos_turn = jnp.cos(phases)[:, :, None]
    sin_turn = jnp.sin(phases)[:, :, None]
    rotated = jnp.stack(
        [real_sum * cos_turn - imag_sum * sin_turn, real_sum * sin_turn + imag_sum * cos_turn]
    )
    target_grid = lax.broadcasted_iota(jnp.int32, (seq_count, 2 * seq_count), 0)
    slot_grid = lax.broadcasted_iota(jnp.int32, (seq_count, 2 * seq_count), 1)
    last_table = angle_of(target_grid * coarse_order(slot_grid, seq_count), 2 * seq_count)
    cos_last = jnp.cos(last_table)
    sin_last = jnp.sin(last_table)
    pieces = lax.all_to_all(rotated, "seq", split_axis=2, concat_axis=1, tiled=True)
    value = contract("sk,krw->srw", cos_last, pieces[0]) - contract(
        "sk,krw->srw", sin_last, pieces[1]
    )
    other = contract("sk,krw->srw", sin_last, pieces[0]) + contract(
        "sk,krw->srw", cos_last, pieces[1]
    )
    gathered = (value / period_len, other / period_len)
    gathered = jnp.concatenate([gathered[0], gathered[1]], axis=2)
    home_rows = lax.all_to_all(gathered, "seq", split_axis=0, concat_axis=1, tiled=True)
    return home_rows.reshape(row_count, home_rows.shape[2])


def invert_all(spectra):
    half_width = spectra.shape[3] // 2
    joined = jnp.stack(
        [
            spectra[0, :, :, :half_width] - spectra[1, :, :, half_width:],
            spectra[1, :, :, :half_width] + spectra[0, :, :, half_width:],
        ]
    )
    return inverse_rows(joined)


def shards(signal, grad_out, filter_taps, skip_gain):
    channels = filter_taps.shape[1]
    signal_rows = signal[0].astype(jnp.float32)
    grad_rows = grad_out[0].astype(jnp.float32)
    tap_half = filter_taps.shape[1] // 2
    columns = jnp.concatenate(
        [signal_rows, filter_taps[:, :tap_half], grad_rows, filter_taps[:, tap_half:]], axis=1
    )
    first, second = split_pairs(forward_spectra(columns))
    signal_spec = first[:, :, :, :channels]
    grad_spec = second[:, :, :, :channels]
    own_spec = jnp.concatenate([first[:, :, :, channels:], second[:, :, :, channels:]], axis=3)
    input_spec = jnp.stack(
        [
            grad_spec[0] * own_spec[0] + grad_spec[1] * own_spec[1],
            grad_spec[1] * own_spec[0] - grad_spec[0] * own_spec[1],
        ]
    )
    filter_terms = jnp.stack(
        [
            grad_spec[0] * signal_spec[0] + grad_spec[1] * signal_spec[1],
            grad_spec[1] * signal_spec[0] - grad_spec[0] * signal_spec[1],
        ]
    )
    summed = lax.psum(filter_terms, "batch")
    rows_back = invert_all(jnp.concatenate([input_spec, summed], axis=3))
    filter_grad = rows_back[:, channels:]
    input_grad = (rows_back[:, :channels] + skip_gain[None, :] * grad_rows).astype(jnp.bfloat16)
    return (input_grad[None], filter_grad)


def solution(mesh):
    return jax.shard_map(
        shards,
        mesh=mesh,
        in_specs=(P("batch", "seq", None), P("batch", "seq", None), P("seq", None), P()),
        out_specs=(P("batch", "seq", None), P("seq", None)),
        check_vma=False,
    )
```

profile of v0, /device:TPU:0, one launch (start us, length us, event | category | flops | bytes accessed | tf_op | source)
XLA Modules:
  0.0 231.8 jit_solution(8577959397815715858)
XLA Ops:
  9.2 1.7 copy.37
  10.9 7.3 %all-to-all-start = ((f32[1,256,768]{2,0,1:T(1,128)}), f32[1,256,768]{2,0,1:T(1,128)S(1)}, u32[]{:S(2)}, u32[]{:S(2)}) async-start(f32[1,256,768]{2,0,1:T(1,128)} %copy.37), calls=%async_computation | async-start | bytes 1572864 | tf_op jit(solution)/shard_map/all_to_all | solution.py:37
  18.4 20.0 %all-to-all-done = f32[1,256,768]{2,0,1:T(1,128)S(1)} async-done(((f32[1,256,768]{2,0,1:T(1,128)}), f32[1,256,768]{2,0,1:T(1,128)S(1)}, u32[]{:S(2)}, u32[]{:S(2)}) %all-to-all-start) | async-done | bytes 786464 | tf_op jit(solution)/shard_map/all_to_all | solution.py:37
  42.7 1.7 copy.40
  44.4 3.6 %all-to-all-start.1 = ((f32[2,16,32,384]{3,2,0,1:T(8,128)}), f32[2,16,32,384]{3,2,0,1:T(8,128)S(1)}, u32[]{:S(2)}, u32[]{:S(2)}) async-start(f32[2,16,32,384]{3,2,0,1:T(8,128)} %copy.40), calls=%async_computation.1 | async-start | bytes 3145728 | tf_op jit(solution)/shard_map/all_to_all | solution.py:71
  48.2 36.9 %all-to-all-done.1 = f32[2,16,32,384]{3,2,0,1:T(8,128)S(1)} async-done(((f32[2,16,32,384]{3,2,0,1:T(8,128)}), f32[2,16,32,384]{3,2,0,1:T(8,128)S(1)}, u32[]{:S(2)}, u32[]{:S(2)}) %all-to-all-start.1) | async-done | bytes 1572896 | tf_op jit(solution)/shard_map/all_to_all | solution.py:71
  85.5 2.2 fusion.36
  87.7 2.2 fusion.34
  89.9 2.2 convolution_subtract_fusion
  92.1 2.2 convolution_add_fusion
  94.3 1.3 pad_maximum_fusion
  95.6 1.3 fusion.4
  96.9 11.2 %rev.4 = f32[2,2,256,384]{2,3,1,0:T(8,128)S(1)} reverse(f32[2,2,256,384]{2,3,1,0:T(8,128)} %pad_maximum_fusion), dimensions={1,2} | reverse | bytes 3145728 | tf_op jit(solution)/shard_map/rev | solution.py:85
  108.1 7.2 %slice.127 = f32[2,1,256,384]{2,3,1,0:T(8,128)} reverse(f32[2,1,256,384]{2,3,1,0:T(8,128)} %get-tuple-element.17), dimensions={2} | reverse | bytes 1572864 | tf_op jit(solution)/shard_map/slice | solution.py:84
  115.3 7.2 %slice.123 = f32[2,1,256,384]{2,3,0,1:T(8,128)} reverse(f32[2,1,256,384]{2,3,0,1:T(8,128)} %get-tuple-element.16), dimensions={2} | reverse | bytes 1572864 | tf_op jit(solution)/shard_map/slice | solution.py:83
  123.8 1.4 maximum_bitcast_fusion.1
  129.7 33.8 %all-reduce.2.cloned.1.call-done = f32[2,2,256,256]{2,3,1,0:T(8,128)} async-done(((f32[2,2,256,256]{2,3,1,0:T(8,128)}), f32[2,2,256,256]{2,3,1,0:T(8,128)}) %all-reduce.2.cloned.1.call-update) | async-done | bytes 1048592 | tf_op jit(solution)/shard_map/psum | solution.py:167
  163.5 1.7 fusion.15
  165.2 1.6 fusion.30
  166.7 1.6 fusion.32
  168.3 1.6 convolution_add_fusion.2
  169.9 1.6 subtract_bitcast_fusion.1
  172.2 30.5 %all_to_all.51 = f32[2,2,256,256]{3,1,0,2:T(2,128)S(1)} all-to-all(f32[2,2,256,256]{3,1,0,2:T(2,128)S(1)} %copy.49), channel_id=1, replica_groups=mesh['batch'=4,'seq'=8] {'seq'}, dimensions={2} | all-to-all | bytes 2097152 | tf_op jit(solution)/shard_map/all_to_all | solution.py:119
  206.7 17.4 %all_to_all.52 = f32[8,32,512]{2,1,0:T(8,128)S(1)} all-to-all(f32[8,32,512]{2,1,0:T(8,128)S(1)} %copy.53), channel_id=1, replica_groups=mesh['batch'=4,'seq'=8] {'seq'}, dimensions={0} | all-to-all | bytes 1048576 | tf_op jit(solution)/shard_map/all_to_all | solution.py:128
  (61 shorter events, 18.1 us)
Async XLA Ops:
  10.9 27.5 %all-to-all-start = ((f32[1,256,768]{2,0,1:T(1,128)}), f32[1,256,768]{2,0,1:T(1,128)S(1)}, u32[]{:S(2)}, u32[]{:S(2)}) async-start(f32[1,256,768]{2,0,1:T(1,128)} %copy.37), calls=%async_computation | async-start | bytes 1572864 | tf_op jit(solution)/shard_map/all_to_all | solution.py:37
  44.4 40.8 %all-to-all-start.1 = ((f32[2,16,32,384]{3,2,0,1:T(8,128)}), f32[2,16,32,384]{3,2,0,1:T(8,128)S(1)}, u32[]{:S(2)}, u32[]{:S(2)}) async-start(f32[2,16,32,384]{3,2,0,1:T(8,128)} %copy.40), calls=%async_computation.1 | async-start | bytes 3145728 | tf_op jit(solution)/shard_map/all_to_all | solution.py:71
  48.0 115.5 %all-reduce.2.cloned.1.call-start = ((), (), s32[]{:S(2)}) async-start(), calls=%async_computation.4 | async-start | bytes 2097152 | tf_op jit(solution)/shard_map/psum | solution.py:167
  122.5 2.6 %copy-start.4 = (f32[2,1,256,384]{2,3,1,0:T(8,128)S(1)}, f32[2,1,256,384]{2,3,1,0:T(8,128)}, u32[]{:S(2)}) copy-start(f32[2,1,256,384]{2,3,1,0:T(8,128)} %slice.127) | copy-start | bytes 2359300
  125.8 0.9 copy-start
  125.8 1.1 copy-start.2
  126.9 1.5 copy-start.1
  126.9 1.7 copy-start.3
  206.3 17.8 %copy-start.5 = (bf16[1,256,256]{2,1,0:T(8,128)(2,1)S(1)}, bf16[1,256,256]{2,1,0:T(8,128)(2,1)}, u32[]{:S(2)}) copy-start(bf16[1,256,256]{2,1,0:T(8,128)(2,1)} %param.5) | copy-start | bytes 393220
  206.4 17.8 %copy-start.6 = (f32[256]{0:T(256)S(1)}, f32[256]{0:T(256)}, u32[]{:S(2)}) copy-start(f32[256]{0:T(256)} %param.7) | copy-start | bytes 3076
Sparse Core Ops, SparseCore 0:
  128.1 35.3 all-reduce.1
where the time goes:
time: 234 us; the launch traced here: 232 us
  waiting for transfers between devices  90.7 us (39%)
  blocking collectives  48 us (21%)
  local copies, waits for them, and re-layouts  36 us (15%)
  matrix products  20.8 us (9%)
  between operations  14.4 us (6%)
  starting transfers between devices  11.1 us (5%)
  other arithmetic  10.9 us (5%)
    all_to_all x1, waiting for transfers between devices, forward_spectra(): lax.all_to_all(rotated, 'seq', split_axis=1, concat_axis=2, tiled=True)  36.9 us
    psum x1, waiting for transfers between devices, shards(): summed = lax.psum(filter_terms, 'batch')  33.8 us
    all_to_all x1, blocking collectives, inverse_rows(): lax.all_to_all(rotated, 'seq', split_axis=2, concat_axis=1, tiled=True)  30.5 us
    dot_general x16, matrix products, contract(): return jnp.einsum(form, table, operand, precision=lax.Precision.HIGHEST)  20.8 us
    all_to_all x1, waiting for transfers between devices, forward_spectra(): lax.all_to_all(columns.reshape(1, row_count, columns.shape[1]), 'seq', sp...  20 us
    all_to_all x1, blocking collectives, inverse_rows(): lax.all_to_all(gathered, 'seq', split_axis=0, concat_axis=1, tiled=True)  17.4 us
    rev x1, local copies, waits for them, and re-layouts, split_pairs(): reversed_q[:, ::-1]  11.2 us
    slice x2, local copies, waits for them, and re-layouts, split_pairs(): zero_row = jnp.roll(reversed_q[:, 0], 1, axis=1)  8.44 us
  transfers between devices with their start and end apart: 3, of which 3 were waited for; matrix products, arithmetic and copies ran while one was open for 1% of the time, Pallas kernels for 0%

commit v1 on v0

--- a/solution.py
+++ b/solution.py
@@ -164,7 +164,9 @@
             grad_spec[1] * signal_spec[0] - grad_spec[0] * signal_spec[1],
         ]
     )
-    summed = lax.psum(filter_terms, "batch")
+    summed = filter_terms
+    for hop in (1, 2):
+        summed = summed + lax.ppermute(summed, "batch", [(dev, dev ^ hop) for dev in range(4)])
     rows_back = invert_all(jnp.concatenate([input_spec, summed], axis=3))
     filter_grad = rows_back[:, channels:]
     input_grad = (rows_back[:, :channels] + skip_gain[None, :] * grad_rows).astype(jnp.bfloat16)

time: 234 us -> 209 us (0.89)
  between operations: 14.4 us -> 1.14 us
  waiting for transfers between devices: 90.7 us -> 82.3 us
  local copies, waits for them, and re-layouts: 36 us -> 33.1 us
    psum x1 -> x0, waiting for transfers between devices: 33.8 us -> none  [shards(): summed = lax.psum(filter_terms, 'batch')]
    ppermute x0 -> x2, waiting for transfers between devices: none -> 25.3 us  [shards(): lax.ppermute(summed, 'batch', [(dev, dev ^ hop) for dev in range(4)])]
    add x0 -> x3, other arithmetic: none -> 2.91 us  [the longest x2 2.7 us: shards(): summed + lax.ppermute(summed, 'batch', [(dev, dev ^ hop) for dev in range...]
    rev x1, local copies, waits for them, and re-layouts: 11.2 us -> 8.72 us  [split_pairs(): reversed_q[:, ::-1]]
  transfers between devices with their start and end apart: 3 -> 4, of which waited for: 3 -> 4; matrix products, arithmetic and copies ran while one was open for 1% -> 1% of each run, Pallas kernels for 0% -> 0%
where the time goes in v1:
time: 209 us; the launch traced here: 207 us
  waiting for transfers between devices  82.3 us (39%)
  blocking collectives  46 us (22%)
  local copies, waits for them, and re-layouts  33.1 us (16%)
  matrix products  20.8 us (10%)
  starting transfers between devices  12.6 us (6%)
  other arithmetic  11.2 us (5%)
    all_to_all x1, waiting for transfers between devices, forward_spectra(): lax.all_to_all(rotated, 'seq', split_axis=1, concat_axis=2, tiled=True)  37.1 us
    all_to_all x1, blocking collectives, inverse_rows(): lax.all_to_all(rotated, 'seq', split_axis=2, concat_axis=1, tiled=True)  28.6 us
    ppermute x2, waiting for transfers between devices, shards(): lax.ppermute(summed, 'batch', [(dev, dev ^ hop) for dev in range(4)])  25.3 us
    dot_general x16, matrix products, contract(): return jnp.einsum(form, table, operand, precision=lax.Precision.HIGHEST)  20.8 us
    all_to_all x1, waiting for transfers between devices, forward_spectra(): lax.all_to_all(columns.reshape(1, row_count, columns.shape[1]), 'seq', sp...  19.9 us
    all_to_all x1, blocking collectives, inverse_rows(): lax.all_to_all(gathered, 'seq', split_axis=0, concat_axis=1, tiled=True)  17.4 us
    rev x1, local copies, waits for them, and re-layouts, split_pairs(): reversed_q[:, ::-1]  8.72 us
    slice x2, local copies, waits for them, and re-layouts, split_pairs(): zero_row = jnp.roll(reversed_q[:, 0], 1, axis=1)  8.36 us
  transfers between devices with their start and end apart: 4, of which 4 were waited for; matrix products, arithmetic and copies ran while one was open for 1% of the time, Pallas kernels for 0%

profile of v1, /device:TPU:0, one launch (start us, length us, event | category | flops | bytes accessed | tf_op | source)
XLA Modules:
  0.0 207.2 jit_solution(7849913168239028641)
XLA Ops:
  2.7 1.7 copy.37
  4.4 7.3 %all-to-all-start = ((f32[1,256,768]{2,0,1:T(1,128)}), f32[1,256,768]{2,0,1:T(1,128)S(1)}, u32[]{:S(2)}, u32[]{:S(2)}) async-start(f32[1,256,768]{2,0,1:T(1,128)} %copy.37), calls=%async_computation | async-start | bytes 1572864 | tf_op jit(solution)/shard_map/all_to_all | solution.py:37
  11.9 19.9 %all-to-all-done = f32[1,256,768]{2,0,1:T(1,128)S(1)} async-done(((f32[1,256,768]{2,0,1:T(1,128)}), f32[1,256,768]{2,0,1:T(1,128)S(1)}, u32[]{:S(2)}, u32[]{:S(2)}) %all-to-all-start) | async-done | bytes 786464 | tf_op jit(solution)/shard_map/all_to_all | solution.py:37
  36.2 1.7 copy.40
  37.8 3.8 %all-to-all-start.1 = ((f32[2,16,32,384]{3,2,0,1:T(8,128)}), f32[2,16,32,384]{3,2,0,1:T(8,128)S(1)}, u32[]{:S(2)}, u32[]{:S(2)}) async-start(f32[2,16,32,384]{3,2,0,1:T(8,128)} %copy.40), calls=%async_computation.1 | async-start | bytes 3145728 | tf_op jit(solution)/shard_map/all_to_all | solution.py:71
  41.6 37.1 %all-to-all-done.1 = f32[2,16,32,384]{3,2,0,1:T(8,128)S(1)} async-done(((f32[2,16,32,384]{3,2,0,1:T(8,128)}), f32[2,16,32,384]{3,2,0,1:T(8,128)S(1)}, u32[]{:S(2)}, u32[]{:S(2)}) %all-to-all-start.1) | async-done | bytes 1572896 | tf_op jit(solution)/shard_map/all_to_all | solution.py:71
  79.0 2.2 %fusion.34 = f32[2,384,256]{2,1,0:T(8,128)S(1)} fusion(f32[2,256,384]{2,1,0:T(8,128)S(1)} %bitcast.152), kind=kOutput, calls=%fused_computation.75 | convolution fusion | flops 604897280 | bytes 1572864 | tf_op jit(solution)/shard_map/qr,krw->kqw/dot_general | solution.py:29
  81.2 2.2 %fusion.36 = f32[2,384,256]{2,1,0:T(8,128)S(1)} fusion(f32[2,256,384]{2,1,0:T(8,128)S(1)} %bitcast.154), kind=kOutput, calls=%fused_computation.77 | convolution fusion | flops 604897280 | bytes 1572864 | tf_op jit(solution)/shard_map/qr,krw->kqw/dot_general | solution.py:29
  83.5 2.2 %convolution_add_fusion = f32[2,384,256]{2,1,0:T(8,128)S(1)} fusion(f32[2,384,256]{2,1,0:T(8,128)S(1)} %fusion.34, f32[2,256,384]{2,1,0:T(8,128)S(1)} %bitcast.155), kind=kOutput, calls=%fused_computation.7 | convolution fusion | flops 605093888 | bytes 2359296 | tf_op jit(solution)/shard_map/qr,krw->kqw/dot_general | solution.py:29
  85.7 2.2 %convolution_subtract_fusion = f32[2,384,256]{2,1,0:T(8,128)S(1)} fusion(f32[2,384,256]{2,1,0:T(8,128)S(1)} %fusion.36, f32[2,256,384]{2,1,0:T(8,128)S(1)} %bitcast.153), kind=kOutput, calls=%fused_computation.8 | convolution fusion | flops 605093888 | bytes 2359296 | tf_op jit(solution)/shard_map/qr,krw->kqw/dot_general | solution.py:29
  89.2 7.2 %slice.123 = f32[2,1,256,384]{2,3,0,1:T(8,128)} reverse(f32[2,1,256,384]{2,3,0,1:T(8,128)} %get-tuple-element.16), dimensions={2} | reverse | bytes 1572864 | tf_op jit(solution)/shard_map/slice | solution.py:83
  97.6 7.2 %slice.127 = f32[2,1,256,384]{2,3,1,0:T(8,128)} reverse(f32[2,1,256,384]{2,3,1,0:T(8,128)} %get-tuple-element.17), dimensions={2} | reverse | bytes 1572864 | tf_op jit(solution)/shard_map/slice | solution.py:84
  104.8 8.7 %rev.4 = f32[2,2,256,384]{2,3,1,0:T(8,128)} reverse(f32[2,2,256,384]{2,3,1,0:T(8,128)S(1)} %pad_maximum_fusion), dimensions={1,2} | reverse | bytes 3145728 | tf_op jit(solution)/shard_map/rev | solution.py:85
  113.5 1.5 maximum_bitcast_fusion.1
  118.2 2.6 %collective-permute-done = f32[2,2,256,256]{2,3,1,0:T(8,128)S(1)} collective-permute-done((f32[2,2,256,256]{2,3,1,0:T(8,128)S(1)}, f32[2,2,256,256]{2,3,1,0:T(8,128)S(1)}, u32[]{:S(2)}, u32[]{:S(2)}) %collective-permute-start) | collective-permute-done | bytes 1048608 | tf_op jit(solution)/shard_map/ppermute | solution.py:169
  122.1 1.5 collective-permute-start.1
  125.0 22.7 %collective-permute-done.1 = f32[2,2,256,256]{2,3,1,0:T(8,128)} collective-permute-done((f32[2,2,256,256]{2,3,1,0:T(8,128)}, f32[2,2,256,256]{2,3,1,0:T(8,128)}, u32[]{:S(2)}, u32[]{:S(2)}) %collective-permute-start.1) | collective-permute-done | bytes 1048608 | tf_op jit(solution)/shard_map/ppermute | solution.py:169
  147.7 1.4 fusion.193
  149.3 1.6 fusion.28
  150.9 1.6 fusion.26
  152.5 1.6 convolution_subtract_fusion.2
  154.0 1.6 subtract_bitcast_fusion.1
  156.4 28.6 %all_to_all.51 = f32[2,2,256,256]{3,1,0,2:T(2,128)S(1)} all-to-all(f32[2,2,256,256]{3,1,0,2:T(2,128)S(1)} %copy.49), channel_id=1, replica_groups=mesh['batch'=4,'seq'=8] {'seq'}, dimensions={2} | all-to-all | bytes 2097152 | tf_op jit(solution)/shard_map/all_to_all | solution.py:119
  189.0 17.4 %all_to_all.52 = f32[8,32,512]{2,1,0:T(8,128)S(1)} all-to-all(f32[8,32,512]{2,1,0:T(8,128)S(1)} %copy.53), channel_id=1, replica_groups=mesh['batch'=4,'seq'=8] {'seq'}, dimensions={0} | all-to-all | bytes 1048576 | tf_op jit(solution)/shard_map/all_to_all | solution.py:128
  (74 shorter events, 20.6 us)
Async XLA Ops:
  4.4 27.5 %all-to-all-start = ((f32[1,256,768]{2,0,1:T(1,128)}), f32[1,256,768]{2,0,1:T(1,128)S(1)}, u32[]{:S(2)}, u32[]{:S(2)}) async-start(f32[1,256,768]{2,0,1:T(1,128)} %copy.37), calls=%async_computation | async-start | bytes 1572864 | tf_op jit(solution)/shard_map/all_to_all | solution.py:37
  11.7 23.2 %copy-start.7 = (s32[16]{0:T(128)}, s32[16]{0:T(128)S(1)}, u32[]{:S(2)}) copy-start(s32[16]{0:T(128)S(1)} %get-tuple-element.38) | copy-start | bytes 196
  11.7 23.2 %copy-start.9 = (s32[16]{0:T(128)}, s32[16]{0:T(128)S(1)}, u32[]{:S(2)}) copy-start(s32[16]{0:T(128)S(1)} %get-tuple-element.39) | copy-start | bytes 196
  37.8 40.8 %all-to-all-start.1 = ((f32[2,16,32,384]{3,2,0,1:T(8,128)}), f32[2,16,32,384]{3,2,0,1:T(8,128)S(1)}, u32[]{:S(2)}, u32[]{:S(2)}) async-start(f32[2,16,32,384]{3,2,0,1:T(8,128)} %copy.40), calls=%async_computation.1 | async-start | bytes 3145728 | tf_op jit(solution)/shard_map/all_to_all | solution.py:71
  113.5 1.6 copy-start
  116.9 0.9 copy-start.1
  116.9 1.1 copy-start.3
  118.1 5.8 %copy-start.2 = (f32[1,2,256,384]{2,3,1,0:T(8,128)S(1)}, f32[1,2,256,384]{2,3,1,0:T(8,128)}, u32[]{:S(2)}) copy-start(f32[1,2,256,384]{2,3,1,0:T(8,128)} %copy-done.1) | copy-start | bytes 2359300
  118.1 2.7 %collective-permute-start = (f32[2,2,256,256]{2,3,1,0:T(8,128)S(1)}, f32[2,2,256,256]{2,3,1,0:T(8,128)S(1)}, u32[]{:S(2)}, u32[]{:S(2)}) collective-permute-start(f32[2,2,256,256]{2,3,1,0:T(8,128)S(1)} %pad_maximum_fusion.3), channel_id=1, source_target_pairs={{0,8},{8,0},{16,24},{24,16},{1,9},{9,1},{17,25},{25,17},{2,10},{10... | collective-permute-start | bytes 3145736 | tf_op jit(solution)/shard_map/ppermute | solution.py:169
  120.8 1.3 copy-start.4
  122.1 25.5 %collective-permute-start.1 = (f32[2,2,256,256]{2,3,1,0:T(8,128)}, f32[2,2,256,256]{2,3,1,0:T(8,128)}, u32[]{:S(2)}, u32[]{:S(2)}) collective-permute-start(f32[2,2,256,256]{2,3,1,0:T(8,128)} %fusion.167), channel_id=1, source_target_pairs={{0,16},{8,24},{16,0},{24,8},{1,17},{9,25},{17,1},{25,9},{2,18},{10... | collective-permute-start | bytes 3145736 | tf_op jit(solution)/shard_map/ppermute | solution.py:169
  123.9 23.8 %copy-start.5 = (f32[2,2,256,256]{2,3,1,0:T(8,128)S(1)}, f32[2,2,256,256]{2,3,1,0:T(8,128)}, u32[]{:S(2)}) copy-start(f32[2,2,256,256]{2,3,1,0:T(8,128)} %copy-done.4) | copy-start | bytes 3145732
  185.3 0.8 copy-start.8
  185.3 0.8 copy-start.10
  188.6 17.8 %copy-start.6 = (bf16[1,256,256]{2,1,0:T(8,128)(2,1)S(1)}, bf16[1,256,256]{2,1,0:T(8,128)(2,1)}, u32[]{:S(2)}) copy-start(bf16[1,256,256]{2,1,0:T(8,128)(2,1)} %param.5) | copy-start | bytes 393220
  188.6 17.8 %copy-start.11 = (f32[256]{0:T(256)S(1)}, f32[256]{0:T(256)}, u32[]{:S(2)}) copy-start(f32[256]{0:T(256)} %param.7) | copy-start | bytes 3076
